TPU v7x, 256 devices: a whole 4x4x8 slice. The times are simulated.
256 devices in a mesh: blk: 256 (over z, x, y, core).
Axes of the slice: x: 4, y: 4, z: 8, core: 2. Of those that a mesh axis runs over, the one named last changes fastest.
Arguments:
- features: bfloat16 [262144, 128], P('blk'), may hold values from -6 to 6
- lengthscale: float32 [128], replicated, may hold values from 4 to 40
- noise_var: float32 [1], replicated, may hold values from 0.5 to 2
- outputscale: float32 [1], replicated, may hold values from 0.03 to 0.1
- solution: float32 [262144, 64], P('blk'), may hold values from -6 to 6
- residual: float32 [262144, 64], P('blk'), may hold values from -36 to 36
- direction: float32 [262144, 64], P('blk'), may hold values from -36 to 36
Outputs:
- new_solution: float32 [262144, 64], P('blk')
- new_residual: float32 [262144, 64], P('blk')
- new_direction: float32 [262144, 64], P('blk')
All inputs are finite; a program needn't handle non-finite values.
Results may differ from a plain program's by a relative error of at most 0.0014.
Values may be sent and summed in bfloat16 or wider, within the bound.
A program may use at most 64 MiB of HBM per device.

v0:
```python
import math

import jax
import jax.numpy as jnp
from jax import lax
from jax.experimental import pallas as pl
from jax.experimental.pallas import tpu as pltpu
from jax.sharding import PartitionSpec as P

AXIS = "blk"
MESH = pl.DeviceIdType.MESH
OWN, P1, M1, P32, M32, M2, P33 = range(7)
CHUNKS = 4
STRIP = 64

RATE = math.sqrt(10.0) * math.log2(math.e)
POLY_P = 3.0 / math.sqrt(10.0)
POLY_Q = 0.3
TINY = 1e-30


def dot(left, right, dims):
    return lax.dot_general(left, right, (dims, ((), ())), preferred_element_type=jnp.float32)


def kernel(
    n_dev, width, features, lengthscale, noise_var, outputscale, direction, residual,
    applied_ref, coef_ref,
    feat, dvec, res, blk, meta, half_col, dt, s0, s1, t0, t1, rhs, acc, acc2, ret_out, ret_in, sums,
    load_sem, x_send, x_recv, m_send, m_recv, r_send, r_recv, a_send, a_recv,
):
    me = lax.axis_index(AXIS)
    pts = width * CHUNKS
    rhs_n = direction.shape[0]
    s_buf, t_buf = (s0, s1), (t0, t1)

    def at(offset):
        return lax.rem(me + (offset + n_dev), n_dev)

    def group_peer(stride, size, k):
        place = lax.rem(me // stride, size)
        return me + (lax.rem(place + k, size) - place) * stride

    stages = ((1, 8), (8, 4), (32, n_dev // 32))
    loads = [
        pltpu.make_async_copy(features, feat, load_sem.at[0]),
        pltpu.make_async_copy(direction, dvec, load_sem.at[1]),
        pltpu.make_async_copy(residual, res, load_sem.at[2]),
    ]
    for load in loads:
        load.start()

    barrier = pltpu.get_barrier_semaphore()
    peers = [at(o) for o in (1, -1, 2, -2, 32, -32, 33, -33)]
    for stride, size in stages:
        peers += [group_peer(stride, size, k) for k in range(1, size)]
    for peer in peers:
        pl.semaphore_signal(barrier, inc=1, device_id=(peer,), device_id_type=MESH)

    def x_copy(from_slot, to_slot, chunk, way, device):
        rows = pl.ds(pl.multiple_of(chunk * width, width), width)
        return pltpu.make_async_remote_copy(
            src_ref=blk.at[from_slot, :, rows, :],
            dst_ref=blk.at[to_slot, :, rows, :],
            send_sem=x_send.at[way, chunk],
            recv_sem=x_recv.at[to_slot, chunk],
            device_id=(device,),
            device_id_type=MESH,
        )

    def m_copy(from_slot, to_slot, way, device):
        return pltpu.make_async_remote_copy(
            src_ref=meta.at[from_slot],
            dst_ref=meta.at[to_slot],
            send_sem=m_send.at[way],
            recv_sem=m_recv.at[to_slot],
            device_id=(device,),
            device_id_type=MESH,
        )

    own_ways = ((0, OWN, M1, 1), (1, OWN, P32, -32), (2, OWN, M32, 32), (3, OWN, P1, -1))
    fwd_m2 = (4, M1, M2, 1)
    fwd_p33 = (5, P32, P33, -1)

    loads[0].wait()
    scaled = (feat[...].astype(jnp.float32) / lengthscale[...]).astype(jnp.bfloat16)
    blk[OWN, 0] = scaled
    exact = scaled.astype(jnp.float32)
    half = 0.5 * jnp.sum(exact * exact, axis=1, keepdims=True)
    half_col[0] = jnp.broadcast_to(half, (pts, 128))
    for r in range(pts // 128):
        meta[OWN, r : r + 1, :] = half_col[0, r * 128 : (r + 1) * 128, :].T[0:1, :]
    loads[1].wait()
    own_d = dvec[...]
    high = own_d.astype(jnp.bfloat16)
    low = (own_d - high.astype(jnp.float32)).astype(jnp.bfloat16)
    blk[OWN, 1] = jnp.concatenate([high, low], axis=0).T

    pl.semaphore_wait(barrier, len(peers))
    for way, src, dst, offset in own_ways:
        m_copy(src, dst, way, at(offset)).start()
    for chunk in range(CHUNKS):
        for way, src, dst, offset in own_ways:
            x_copy(src, dst, chunk, way, at(offset)).start()

    def gram(left_slot, slot, chunk, par):
        rows = pl.ds(pl.multiple_of(chunk * width, width), width)
        s_buf[par][...] = dot(blk[left_slot, 0], blk[slot, 0, rows, :], ((1,), (1,)))

    def elem(half_slot, slot, chunk, par):
        for h in range(width // 128):
            row = meta[slot, pl.ds(chunk * (width // 128) + h, 1), :]
            for strip in range(pts // STRIP):
                rows = slice(strip * STRIP, (strip + 1) * STRIP)
                lanes = slice(h * 128, (h + 1) * 128)
                u = (half_col[half_slot, rows, :] + row) - s_buf[par][rows, lanes]
                u = jnp.maximum(u, TINY)
                r = u * lax.rsqrt(u)
                value = ((r + POLY_P) * r + POLY_Q) * jnp.exp2(r * (-RATE))
                top = value.astype(jnp.bfloat16)
                rest = (value - top.astype(jnp.float32)).astype(jnp.bfloat16)
                t_buf[par][rows, lanes] = top
                t_buf[par][rows, slice(width + h * 128, width + (h + 1) * 128)] = rest

    def forward(total, slot, chunk, par):
        rows = pl.ds(pl.multiple_of(chunk * width, width), width)
        vec = blk[slot, 1, rows, :]
        lane = lax.broadcasted_iota(jnp.int32, vec.shape, 1)
        top_only = jnp.where(lane < rhs_n, vec.astype(jnp.float32), 0.0).astype(jnp.bfloat16)
        both = jnp.concatenate([vec, top_only], axis=0)
        total[...] += dot(t_buf[par][...], both, ((1,), (0,)))

    def backward(which, chunk, par):
        full = dot(dt[...], t_buf[par][:, :width], ((1,), (0,)))
        rest = dot(dt[:rhs_n, :], t_buf[par][:, width:], ((1,), (0,)))
        ret_out[which, chunk] = full[:rhs_n] + full[rhs_n:] + rest

    def transposed(total):
        turned = total[...].T
        return turned[:rhs_n] + turned[rhs_n:]

    acc[...] = jnp.zeros_like(acc)
    t1[...] = jnp.zeros_like(t1)
    tiles = 5
    steps = tiles * CHUNKS

    def arrive(step):
        slot = step // CHUNKS
        chunk = lax.rem(step, CHUNKS)

        @pl.when(jnp.logical_and(slot >= 1, slot < tiles))
        def _():
            @pl.when(chunk == 0)
            def _():
                m_copy(OWN, slot, 0, me).wait_recv()

            x_copy(OWN, slot, chunk, 0, me).wait_recv()
            for there in (fwd_m2, fwd_p33):
                way, src, dst, offset = there

                @pl.when(slot == src)
                def _():
                    @pl.when(chunk == 0)
                    def _():
                        m_copy(src, dst, way, at(offset)).start()

                    x_copy(src, dst, chunk, way, at(offset)).start()

    gram(OWN, OWN, 0, 0)

    @pl.loop(0, steps // 2)
    def _(pair):
        arrive(2 * pair + 1)
        arrive(2 * pair + 2)
        for par in (0, 1):
            step = 2 * pair + par
            after = lax.rem(step + 1, steps)
            before = jnp.maximum(step - 1, 0)
            gram(OWN, after // CHUNKS, lax.rem(after, CHUNKS), 1 - par)
            elem(0, step // CHUNKS, lax.rem(step, CHUNKS), par)
            forward(acc, before // CHUNKS, lax.rem(before, CHUNKS), 1 - par)

    forward(acc, tiles - 1, CHUNKS - 1, 1)

    for which, left_slot, slot, back_to, ahead_to in ((0, M2, P1, 1, -2), (1, M32, P33, 33, -32)):
        late = M2 if which == 0 else P33
        m_copy(OWN, late, 0, me).wait_recv()
        for chunk in range(CHUNKS):
            x_copy(OWN, late, chunk, 0, me).wait_recv()
        for r in range(pts // 128):
            half_col[1, r * 128 : (r + 1) * 128, :] = jnp.broadcast_to(
                meta[left_slot, r : r + 1, :], (128, 128)
            ).T
        dt[...] = blk[left_slot, 1].T
        acc2[...] = jnp.zeros_like(acc2)
        gram(left_slot, slot, 0, 0)
        for chunk in range(CHUNKS):
            par = chunk % 2
            if chunk + 1 < CHUNKS:
                gram(left_slot, slot, chunk + 1, 1 - par)
            elem(1, slot, chunk, par)
            if chunk > 0:
                forward(acc2, slot, chunk - 1, 1 - par)
                backward(2 * which, chunk - 1, 1 - par)
        forward(acc2, slot, CHUNKS - 1, (CHUNKS - 1) % 2)
        backward(2 * which, CHUNKS - 1, (CHUNKS - 1) % 2)
        ahead = transposed(acc2)
        for chunk in range(CHUNKS):
            ret_out[2 * which + 1, chunk] = ahead[:, chunk * width : (chunk + 1) * width]
        for kind, offset in ((2 * which, back_to), (2 * which + 1, ahead_to)):
            pltpu.make_async_remote_copy(
                src_ref=ret_out.at[kind],
                dst_ref=ret_in.at[kind],
                send_sem=r_send.at[kind],
                recv_sem=r_recv.at[kind],
                device_id=(at(offset),),
                device_id_type=MESH,
            ).start()

    def ret_copy(kind):
        return pltpu.make_async_remote_copy(
            src_ref=ret_out.at[kind],
            dst_ref=ret_in.at[kind],
            send_sem=r_send.at[kind],
            recv_sem=r_recv.at[kind],
            device_id=(me,),
            device_id_type=MESH,
        )

    own_part = transposed(acc)
    for kind in range(4):
        ret_copy(kind).wait_recv()
    loads[2].wait()
    scale = outputscale[0] * (10.0 / 3.0)
    noise = noise_var[0]
    lane_sums = [jnp.zeros((rhs_n, 128), jnp.float32)] * 4
    for chunk in range(CHUNKS):
        lanes = slice(chunk * width, (chunk + 1) * width)
        there = ret_in[0, chunk] + ret_in[1, chunk] + ret_in[2, chunk] + ret_in[3, chunk]
        vec, old = dvec[:, lanes], res[:, lanes]
        applied = noise * vec + scale * (own_part[:, lanes] + there)
        applied_ref[:, lanes] = applied
        for at_sum, term in enumerate((old * old, vec * applied, old * applied, applied * applied)):
            for h in range(width // 128):
                lane_sums[at_sum] = lane_sums[at_sum] + term[:, h * 128 : (h + 1) * 128]
    rows = [
        jnp.sum(jnp.concatenate(lane_sums[2 * i : 2 * i + 2], axis=0).T, axis=0, keepdims=True)
        for i in range(2)
    ]
    running = jnp.concatenate(rows + [jnp.zeros((6, 128), jnp.float32)], axis=0)

    base = 0
    for stride, size in stages:
        sums[base] = running
        place = lax.rem(me // stride, size)
        copies = []
        for k in range(1, size):
            copies.append(pltpu.make_async_remote_copy(
                src_ref=sums.at[base],
                dst_ref=sums.at[base + k],
                send_sem=a_send.at[base + k],
                recv_sem=a_recv.at[base + k],
                device_id=(group_peer(stride, size, k),),
                device_id_type=MESH,
            ))
        for copy in copies:
            copy.start()
        for copy in copies:
            copy.wait_recv()
        parts = [sums[base + lax.rem(place - member + size, size)] for member in range(size)]
        running = parts[0]
        for part in parts[1:]:
            running = running + part
        base += size

    mean = running * (1.0 / (n_dev * pts))
    swapped = pltpu.roll(mean, 64, 1)
    old_norm, curvature = mean[0:1], swapped[0:1]
    cross_term, applied_norm = mean[1:2], swapped[1:2]
    step_size = old_norm / jnp.maximum(curvature, 1.0)
    updated = old_norm - 2.0 * step_size * cross_term + step_size * step_size * applied_norm
    ratio = updated / (old_norm + 1e-6)
    for i, value in enumerate((step_size, ratio)):
        coef_ref[:, i * 128 : (i + 1) * 128] = jnp.broadcast_to(value, (128, 128)).T[:rhs_n]

    for way, src, dst, offset in own_ways + (fwd_m2, fwd_p33):
        m_copy(src, dst, way, me).wait_send()
        for chunk in range(CHUNKS):
            x_copy(src, dst, chunk, way, me).wait_send()
    for kind in range(4):
        ret_copy(kind).wait_send()
    base = 0
    for stride, size in stages:
        for k in range(1, size):
            pltpu.make_async_remote_copy(
                src_ref=sums.at[base],
                dst_ref=sums.at[base + k],
                send_sem=a_send.at[base + k],
                recv_sem=a_recv.at[base + k],
                device_id=(me,),
                device_id_type=MESH,
            ).wait_send()
        base += size


def local(n_dev, features, lengthscale, noise_var, outputscale, solution, residual, direction):
    pts, feat_n = features.shape
    rhs_n = direction.shape[1]
    width = pts // CHUNKS
    f32, bf16 = jnp.float32, jnp.bfloat16
    dma = pltpu.SemaphoreType.DMA
    in_place = pl.BlockSpec(memory_space=pl.ANY)
    vmem = pl.BlockSpec(memory_space=pltpu.VMEM)
    smem = pl.BlockSpec(memory_space=pltpu.SMEM)
    n_sums = 8 + 4 + n_dev // 32

    def body(*refs):
        kernel(n_dev, width, *refs)

    applied, coef = pl.pallas_call(
        body,
        out_shape=(
            jax.ShapeDtypeStruct((rhs_n, pts), f32),
            jax.ShapeDtypeStruct((rhs_n, 256), f32),
        ),
        in_specs=[in_place, vmem, smem, smem, in_place, in_place],
        out_specs=(vmem, vmem),
        scratch_shapes=[
            pltpu.VMEM((pts, feat_n), bf16),
            pltpu.VMEM((rhs_n, pts), f32),
            pltpu.VMEM((rhs_n, pts), f32),
            pltpu.VMEM((7, 2, pts, 128), bf16),
            pltpu.VMEM((7, 8, 128), f32),
            pltpu.VMEM((2, pts, 128), f32),
            pltpu.VMEM((2 * rhs_n, pts), bf16),
            pltpu.VMEM((pts, width), f32),
            pltpu.VMEM((pts, width), f32),
            pltpu.VMEM((pts, 2 * width), bf16),
            pltpu.VMEM((pts, 2 * width), bf16),
            pltpu.VMEM((2 * width, 128), bf16),
            pltpu.VMEM((pts, 128), f32),
            pltpu.VMEM((pts, 128), f32),
            pltpu.VMEM((4, CHUNKS, rhs_n, width), f32),
            pltpu.VMEM((4, CHUNKS, rhs_n, width), f32),
            pltpu.VMEM((n_sums, 8, 128), f32),
            dma((3,)),
            dma((6, CHUNKS)),
            dma((7, CHUNKS)),
            dma((6,)),
            dma((7,)),
            dma((4,)),
            dma((4,)),
            dma((n_sums,)),
            dma((n_sums,)),
        ],
        compiler_params=pltpu.CompilerParams(
            collective_id=0, has_side_effects=True, vmem_limit_bytes=48 * 1024 * 1024
        ),
        name="cg_step",
    )(features, lengthscale.reshape(1, feat_n), noise_var, outputscale, direction.T, residual.T)
    applied = applied.T
    step_size, ratio = coef[:, 0], coef[:, 128]
    new_solution = solution + step_size[None, :] * direction
    new_residual = residual - step_size[None, :] * applied
    new_direction = new_residual + ratio[None, :] * direction
    return (new_solution, new_residual, new_direction)


def solution(mesh):
    n_dev = mesh.shape[AXIS]
    rows = P(AXIS, None)

    def whole(*arrays):
        return local(n_dev, *arrays)

    return jax.shard_map(
        whole,
        mesh=mesh,
        in_specs=(rows, P(), P(), P(), rows, rows, rows),
        out_specs=(rows, rows, rows),
        check_vma=False,
    )
```

profile of v0, /device:TPU:12, one launch (start us, length us, event | category | flops | bytes accessed | tf_op | source)
XLA Modules:
  0.0 78.1 jit_solution(9870246933378742180)
XLA Ops:
  1.9 0.0 copy-start.3
  1.9 0.6 copy-done.3
  2.6 0.0 copy-start
  2.6 0.9 %copy-done = f32[1024,64]{0,1:T(8,128)S(1)} copy-done((f32[1024,64]{0,1:T(8,128)S(1)}, f32[1024,64]{0,1:T(8,128)}, u32[]{:S(2)}) %copy-start) | copy-done | bytes 262168
  3.5 0.0 copy-start.1
  3.5 0.9 %copy-done.1 = f32[1024,64]{0,1:T(8,128)S(1)} copy-done((f32[1024,64]{0,1:T(8,128)S(1)}, f32[1024,64]{0,1:T(8,128)}, u32[]{:S(2)}) %copy-start.1) | copy-done | bytes 262168
  4.5 0.0 copy-start.2
  4.5 0.9 %copy-done.2 = bf16[1024,128]{1,0:T(8,128)(2,1)S(1)} copy-done((bf16[1024,128]{1,0:T(8,128)(2,1)S(1)}, bf16[1024,128]{1,0:T(8,128)(2,1)}, u32[]{:S(2)}) %copy-start.2) | copy-done | bytes 262168
  5.4 0.0 copy-start.4
  5.4 71.5 %cg_step.1 = (f32[64,1024]{1,0:T(8,128)S(1)}, f32[64,256]{1,0:T(8,128)S(1)}) custom-call(bf16[1024,128]{1,0:T(8,128)(2,1)S(1)} %copy-done.2, f32[1,128]{1,0:T(1,128)S(1)} %bitcast.8, f32[1]{0:T(128)S(6)} %copy.10.refs_2_, f32[1]{0:T(128)S(6)} %copy.11.refs_3_, f32[64,1024]{1,0:T(8,128)S(1)} %bitcast.6, f32[64,1024]{1,0:T(8,128)S(1)} %bitcast.7), custom_call_target="tpu_custom_call" | custom-call | tf_op jit(solution)/shard_map/cg_step/pallas_call | solution.py:320
  77.0 0.1 slice_reduce_fusion
  77.1 0.0 copy-done.4
  77.1 1.0 %multiply_add_fusion = (f32[1024,64]{0,1:T(8,128)}, f32[1024,64]{0,1:T(8,128)}, f32[1024,64]{0,1:T(8,128)}) fusion(f32[1024,64]{0,1:T(8,128)S(1)} %copy-done, f32[64]{0:T(128)S(1)} %get-tuple-element.7, f32[1024,64]{0,1:T(8,128)S(1)} %copy-done.1, f32[64,1024]{1,0:T(8,128)S(1)} %get-tuple-element.6, f32[64]{0:T(128)S(1)} %get-tuple-element.8, ...), kind=kLoop, calls=%fused_computation.1 | loop fusion | flops 393216 | bytes 1835520 | tf_op jit(solution)/shard_map/add | solution.py:365
Async XLA Ops:
  1.9 0.7 copy-start.3
  2.6 0.9 %copy-start = (f32[1024,64]{0,1:T(8,128)S(1)}, f32[1024,64]{0,1:T(8,128)}, u32[]{:S(2)}) copy-start(f32[1024,64]{0,1:T(8,128)} %param.13) | copy-start | bytes 786436
  3.5 0.9 %copy-start.1 = (f32[1024,64]{0,1:T(8,128)S(1)}, f32[1024,64]{0,1:T(8,128)}, u32[]{:S(2)}) copy-start(f32[1024,64]{0,1:T(8,128)} %param.12) | copy-start | bytes 786436
  4.5 0.9 %copy-start.2 = (bf16[1024,128]{1,0:T(8,128)(2,1)S(1)}, bf16[1024,128]{1,0:T(8,128)(2,1)}, u32[]{:S(2)}) copy-start(bf16[1024,128]{1,0:T(8,128)(2,1)} %refs_0_.1) | copy-start | bytes 786436
  5.4 71.6 %copy-start.4 = (f32[1024,64]{0,1:T(8,128)S(1)}, f32[1024,64]{0,1:T(8,128)}, u32[]{:S(2)}) copy-start(f32[1024,64]{0,1:T(8,128)} %param.11) | copy-start | bytes 786436
where the time goes:
time: 78.3 us; the launch traced here: 78.1 us
  Pallas kernels  71.5 us (91%)
  local copies, waits for them, and re-layouts  3.61 us (5%)
  between operations  1.95 us (2%)
  other arithmetic  1.02 us (1%)
    pallas_call x1, Pallas kernels, local(): pl.pallas_call(body, out_shape=(jax.ShapeDtypeStruct((rhs_n, pts), f32),...  71.5 us
    unnamed x10, local copies, waits for them, and re-layouts  3.5 us

commit v1 on v0

v1 whole, which is shorter than its diff:
```python
import math

import jax
import jax.numpy as jnp
from jax import lax
from jax.experimental import pallas as pl
from jax.experimental.pallas import tpu as pltpu
from jax.sharding import PartitionSpec as P

AXIS = "blk"
MESH = pl.DeviceIdType.MESH
OWN, P1, M1, P32, M32, M2, P33 = range(7)
CHUNKS = 4
PLANE = 32
SPAN = 120.0
STRIP = 64

RATE = math.sqrt(10.0) * math.log2(math.e)
POLY_P = 3.0 / math.sqrt(10.0)
POLY_Q = 0.3
TINY = 1e-30


def dot(left, right, dims):
    return lax.dot_general(left, right, (dims, ((), ())), preferred_element_type=jnp.float32)


def kernel(
    n_dev, width, features, lengthscale, noise_var, outputscale, direction, residual,
    applied_ref, coef_ref,
    feat, dvec, res, xbuf, dbuf, meta, half_col, dt, s0, s1, t0, t1, acc, acc2, ret_out, ret_in, sums,
    load_sem, x_send, x_recv, d_send, d_recv, m_send, m_recv, r_send, r_recv, a_send, a_recv,
):
    me = lax.axis_index(AXIS)
    pts = width * CHUNKS
    part = width // 2
    rhs_n = direction.shape[0]
    s_buf, t_buf = (s0, s1), (t0, t1)
    in_plane = lax.rem(me, PLANE)

    def at(offset):
        return lax.rem(me + (offset + n_dev), n_dev)

    def group_peer(stride, size, k):
        place = lax.rem(me // stride, size)
        return me + (lax.rem(place + k, size) - place) * stride

    stages = ((1, 8), (8, 4), (32, n_dev // 32))
    loads = [
        pltpu.make_async_copy(features, feat, load_sem.at[0]),
        pltpu.make_async_copy(direction, dvec, load_sem.at[1]),
        pltpu.make_async_copy(residual, res, load_sem.at[2]),
    ]
    for load in loads:
        load.start()

    barrier = pltpu.get_barrier_semaphore()
    peers = [at(o) for o in (1, -1, 2, -2, 32, -32, 33, -33)]
    peers += [group_peer(1, PLANE, k) for k in (1, 2, PLANE - 1, PLANE - 2)]
    for stride, size in stages:
        peers += [group_peer(stride, size, k) for k in range(1, size)]
    for peer in peers:
        pl.semaphore_signal(barrier, inc=1, device_id=(peer,), device_id_type=MESH)

    last = PLANE - 1
    ways = (
        (OWN, P32, -32, None),
        (OWN, M32, 32, None),
        (OWN, P1, -1, in_plane != 0),
        (OWN, M1, 1, in_plane != last),
        (P32, P33, -1, None),
        (M1, M2, 1, in_plane != last),
        (P32, P1, last, in_plane == 0),
        (M32, M1, -last, in_plane == last),
        (M32, M2, 1 - last, in_plane == last - 1),
    )

    def block_copies(way, chunk):
        src, dst, offset, _ = ways[way]
        rows = pl.ds(pl.multiple_of(chunk * width, width), width)
        device = (at(offset),)
        return (
            pltpu.make_async_remote_copy(
                src_ref=xbuf.at[src, rows, :],
                dst_ref=xbuf.at[dst, rows, :],
                send_sem=x_send.at[way, chunk],
                recv_sem=x_recv.at[dst, chunk],
                device_id=device,
                device_id_type=MESH,
            ),
            pltpu.make_async_remote_copy(
                src_ref=dbuf.at[src, chunk],
                dst_ref=dbuf.at[dst, chunk],
                send_sem=d_send.at[way, chunk],
                recv_sem=d_recv.at[dst, chunk],
                device_id=device,
                device_id_type=MESH,
            ),
        )

    def meta_copy(way):
        src, dst, offset, _ = ways[way]
        return pltpu.make_async_remote_copy(
            src_ref=meta.at[src],
            dst_ref=meta.at[dst],
            send_sem=m_send.at[way],
            recv_sem=m_recv.at[dst],
            device_id=(at(offset),),
            device_id_type=MESH,
        )

    def where_sent(way, action):
        if ways[way][3] is None:
            action()
        else:
            pl.when(ways[way][3])(action)

    def send_chunk(way, chunk, with_meta):
        def go():
            if with_meta is True:
                meta_copy(way).start()
            elif with_meta is not False:
                pl.when(with_meta)(lambda: meta_copy(way).start())
            for copy in block_copies(way, chunk):
                copy.start()

        where_sent(way, go)

    first_way = {dst: way for way, (_, dst, _, _) in reversed(list(enumerate(ways)))}

    def got_chunk(slot, chunk):
        for copy in block_copies(first_way[slot], chunk):
            copy.wait_recv()

    def got_meta(slot):
        meta_copy(first_way[slot]).wait_recv()

    def encode(packed):
        most = jnp.maximum(jnp.max(jnp.abs(packed), axis=0, keepdims=True), TINY)
        power = jnp.floor(jnp.log2(SPAN / most))
        times = jnp.exp2(power).astype(jnp.bfloat16).astype(jnp.float32)
        back = jnp.broadcast_to(jnp.exp2(-power), (16, 128))
        return jnp.exp2(packed * times).astype(jnp.bfloat16), back.astype(jnp.bfloat16)

    def decode(ref):
        back = ref[part:, :].astype(jnp.float32)[0:1]
        return jnp.log(ref[:part, :].astype(jnp.float32)) * (back * (1.0 / math.log(2.0)))

    def low_lanes(shape):
        return lax.broadcasted_iota(jnp.int32, shape, 1) < rhs_n

    def vectors(slot, chunk):
        value = decode(dbuf.at[slot, chunk])
        high = value.astype(jnp.bfloat16).astype(jnp.float32)
        low = value - high
        high_r, low_r = pltpu.roll(high, rhs_n, 1), pltpu.roll(low, rhs_n, 1)
        left = low_lanes(value.shape)
        both = jnp.concatenate([jnp.where(left, high, low_r), jnp.where(left, high_r, low)], axis=0)
        top = jnp.concatenate([jnp.where(left, high, 0.0), jnp.where(left, high_r, 0.0)], axis=0)
        return both.astype(jnp.bfloat16), top.astype(jnp.bfloat16)

    def pack_rows(block):
        return jnp.concatenate([block[:, :part], block[:, part:]], axis=0).T

    loads[0].wait()
    scaled = (feat[...].astype(jnp.float32) / lengthscale[...]).astype(jnp.bfloat16)
    xbuf[OWN] = scaled
    exact = scaled.astype(jnp.float32)
    half = 0.5 * jnp.sum(exact * exact, axis=1, keepdims=True)
    half_col[0] = jnp.broadcast_to(half, (pts, 128))
    for r in range(pts // 128):
        meta[OWN, r : r + 1, :] = half_col[0, r * 128 : (r + 1) * 128, :].T[0:1, :]
    loads[1].wait()
    for chunk in range(CHUNKS):
        code, back = encode(pack_rows(dvec[:, chunk * width : (chunk + 1) * width]))
        dbuf[OWN, chunk, :part] = code
        dbuf[OWN, chunk, part:] = back

    pl.semaphore_wait(barrier, len(peers))
    for chunk in range(CHUNKS):
        for way in range(4):
            send_chunk(way, chunk, chunk == 0)

    def gram(left_slot, slot, chunk, par):
        rows = pl.ds(pl.multiple_of(chunk * width, width), width)
        s_buf[par][...] = dot(xbuf[left_slot], xbuf[slot, rows, :], ((1,), (1,)))

    def elem(half_slot, slot, chunk, par):
        for h in range(width // 128):
            row = meta[slot, pl.ds(chunk * (width // 128) + h, 1), :]
            for strip in range(pts // STRIP):
                rows = slice(strip * STRIP, (strip + 1) * STRIP)
                lanes = slice(h * 128, (h + 1) * 128)
                u = (half_col[half_slot, rows, :] + row) - s_buf[par][rows, lanes]
                u = jnp.maximum(u, TINY)
                r = u * lax.rsqrt(u)
                value = ((r + POLY_P) * r + POLY_Q) * jnp.exp2(r * (-RATE))
                top = value.astype(jnp.bfloat16)
                rest = (value - top.astype(jnp.float32)).astype(jnp.bfloat16)
                t_buf[par][rows, lanes] = top
                t_buf[par][rows, slice(width + h * 128, width + (h + 1) * 128)] = rest

    def forward(total, slot, chunk, par):
        both, top = vectors(slot, chunk)
        total[...] += dot(t_buf[par][...], jnp.concatenate([both, top], axis=0), ((1,), (0,)))

    def backward(kind, chunk, par):
        full = dot(dt[...], t_buf[par][:, :width], ((1,), (0,)))
        rest = dot(dt[:rhs_n, :], t_buf[par][:, width:], ((1,), (0,)))
        code, back = encode(pack_rows(full[:rhs_n] + full[rhs_n:] + rest))
        ret_out[kind, chunk, :part] = code
        ret_out[kind, chunk, part:] = back

    def ret_copy(kind, chunk, offset=1):
        return pltpu.make_async_remote_copy(
            src_ref=ret_out.at[kind, chunk],
            dst_ref=ret_in.at[kind, chunk],
            send_sem=r_send.at[kind, chunk],
            recv_sem=r_recv.at[kind, chunk],
            device_id=(at(offset),),
            device_id_type=MESH,
        )

    def transposed(total):
        turned = total[...].T
        return turned[:rhs_n] + turned[rhs_n:]

    def run(left_slot, half_slot, steps, place, total, each_pair=None, kind=None):
        t1[...] = jnp.zeros_like(t1)
        gram(left_slot, *place(0), 0)

        @pl.loop(0, steps // 2)
        def _(pair):
            if each_pair is not None:
                each_pair(pair)
            for par in (0, 1):
                step = 2 * pair + par
                gram(left_slot, *place(lax.rem(step + 1, steps)), 1 - par)
                elem(half_slot, *place(step), par)
                before = place(jnp.maximum(step - 1, 0))
                forward(total, *before, 1 - par)
                if kind is not None:
                    backward(kind, before[1], 1 - par)

        final = place(steps - 1)
        forward(total, *final, 1)
        if kind is not None:
            backward(kind, final[1], 1)

    acc[...] = jnp.zeros_like(acc)

    def first_place(step):
        later = (step - CHUNKS) // 2
        if isinstance(step, int):
            return (OWN, step) if step < CHUNKS else (P32 + step % 2, later)
        own = step < CHUNKS
        return jnp.where(own, OWN, P32 + lax.rem(step, 2)), jnp.where(own, step, later)

    def pass_on(slot, chunk, with_meta):
        got_chunk(slot, chunk)
        for way, (src, _, _, _) in enumerate(ways):
            if src == slot:
                send_chunk(way, chunk, with_meta)

    def first_arrivals(pair):
        for slot, lag in ((P32, 1), (M32, 2), (M1, 3)):
            chunk = pair - lag

            @pl.when(jnp.logical_and(chunk >= 0, chunk < CHUNKS))
            def _():
                pl.when(chunk == 0)(lambda: got_meta(slot))
                pass_on(slot, chunk, chunk == 0)

    run(OWN, 0, 3 * CHUNKS, first_place, acc, first_arrivals)
    pass_on(M1, CHUNKS - 1, False)

    for kind, left_slot, slot, back_to, ahead_to in ((0, M32, P33, 33, -32), (2, M2, P1, 1, -2)):
        for late in (P33,) if kind == 0 else (M2, P1):
            got_meta(late)
            for chunk in range(CHUNKS):
                got_chunk(late, chunk)
        for r in range(pts // 128):
            half_col[1, r * 128 : (r + 1) * 128, :] = jnp.broadcast_to(
                meta[left_slot, r : r + 1, :], (128, 128)
            ).T
        for chunk in range(CHUNKS):
            dt[:, chunk * width : (chunk + 1) * width] = vectors(left_slot, chunk)[0].T
        acc2[...] = jnp.zeros_like(acc2)
        run(left_slot, 1, CHUNKS, lambda step, slot=slot: (slot, step), acc2, None, kind)
        for chunk in range(CHUNKS):
            ahead = acc2[chunk * width : (chunk + 1) * width, :]
            ahead = ahead + pltpu.roll(ahead, rhs_n, 1)
            ahead = jnp.where(low_lanes((part, 128)), ahead[:part], ahead[part:])
            code, back = encode(ahead)
            ret_out[kind + 1, chunk, :part] = code
            ret_out[kind + 1, chunk, part:] = back
            ret_copy(kind, chunk, back_to).start()
            ret_copy(kind + 1, chunk, ahead_to).start()

    def last_place(step):
        return step // CHUNKS + P1, step % CHUNKS if isinstance(step, int) else lax.rem(step, CHUNKS)

    run(OWN, 0, 2 * CHUNKS, last_place, acc)

    for kind in range(4):
        for chunk in range(CHUNKS):
            ret_copy(kind, chunk).wait_recv()
    for chunk in range(CHUNKS):
        there = decode(ret_in.at[0, chunk])
        for kind in range(1, 4):
            there = there + decode(ret_in.at[kind, chunk])
        left = low_lanes(there.shape)
        acc[chunk * width : chunk * width + part, :] += jnp.where(left, there, 0.0)
        acc[chunk * width + part : (chunk + 1) * width, :] += jnp.where(left, 0.0, there)
    own_part = transposed(acc)
    loads[2].wait()
    scale = outputscale[0] * (10.0 / 3.0)
    noise = noise_var[0]
    lane_sums = [jnp.zeros((rhs_n, 128), jnp.float32)] * 4
    for chunk in range(CHUNKS):
        lanes = slice(chunk * width, (chunk + 1) * width)
        vec, old = dvec[:, lanes], res[:, lanes]
        applied = noise * vec + scale * own_part[:, lanes]
        applied_ref[:, lanes] = applied
        for at_sum, term in enumerate((old * old, vec * applied, old * applied, applied * applied)):
            for h in range(width // 128):
                lane_sums[at_sum] = lane_sums[at_sum] + term[:, h * 128 : (h + 1) * 128]
    rows = [
        jnp.sum(jnp.concatenate(lane_sums[2 * i : 2 * i + 2], axis=0).T, axis=0, keepdims=True)
        for i in range(2)
    ]
    running = jnp.concatenate(rows + [jnp.zeros((6, 128), jnp.float32)], axis=0)

    base = 0
    for stride, size in stages:
        sums[base] = running
        place = lax.rem(me // stride, size)
        copies = []
        for k in range(1, size):
            copies.append(pltpu.make_async_remote_copy(
                src_ref=sums.at[base],
                dst_ref=sums.at[base + k],
                send_sem=a_send.at[base + k],
                recv_sem=a_recv.at[base + k],
                device_id=(group_peer(stride, size, k),),
                device_id_type=MESH,
            ))
        for copy in copies:
            copy.start()
        for copy in copies:
            copy.wait_recv()
        parts = [sums[base + lax.rem(place - member + size, size)] for member in range(size)]
        running = parts[0]
        for part in parts[1:]:
            running = running + part
        base += size

    mean = running * (1.0 / (n_dev * pts))
    swapped = pltpu.roll(mean, 64, 1)
    old_norm, curvature = mean[0:1], swapped[0:1]
    cross_term, applied_norm = mean[1:2], swapped[1:2]
    step_size = old_norm / jnp.maximum(curvature, 1.0)
    updated = old_norm - 2.0 * step_size * cross_term + step_size * step_size * applied_norm
    ratio = updated / (old_norm + 1e-6)
    for i, value in enumerate((step_size, ratio)):
        coef_ref[:, i * 128 : (i + 1) * 128] = jnp.broadcast_to(value, (128, 128)).T[:rhs_n]

    for way in range(len(ways)):
        def left(way=way):
            meta_copy(way).wait_send()
            for chunk in range(CHUNKS):
                for copy in block_copies(way, chunk):
                    copy.wait_send()

        where_sent(way, left)
    for kind in range(4):
        for chunk in range(CHUNKS):
            ret_copy(kind, chunk).wait_send()
    base = 0
    for stride, size in stages:
        for k in range(1, size):
            pltpu.make_async_remote_copy(
                src_ref=sums.at[base],
                dst_ref=sums.at[base + k],
                send_sem=a_send.at[base + k],
                recv_sem=a_recv.at[base + k],
                device_id=(me,),
                device_id_type=MESH,
            ).wait_send()
        base += size


def local(n_dev, features, lengthscale, noise_var, outputscale, solution, residual, direction):
    pts, feat_n = features.shape
    rhs_n = direction.shape[1]
    width = pts // CHUNKS
    f32, bf16 = jnp.float32, jnp.bfloat16
    dma = pltpu.SemaphoreType.DMA
    in_place = pl.BlockSpec(memory_space=pltpu.HBM)
    vmem = pl.BlockSpec(memory_space=pltpu.VMEM)
    smem = pl.BlockSpec(memory_space=pltpu.SMEM)
    n_sums = 8 + 4 + n_dev // 32

    def body(*refs):
        kernel(n_dev, width, *refs)

    applied, coef = pl.pallas_call(
        body,
        out_shape=(
            jax.ShapeDtypeStruct((rhs_n, pts), f32),
            jax.ShapeDtypeStruct((rhs_n, 256), f32),
        ),
        in_specs=[in_place, vmem, smem, smem, in_place, in_place],
        out_specs=(vmem, vmem),
        scratch_shapes=[
            pltpu.VMEM((pts, feat_n), bf16),
            pltpu.VMEM((rhs_n, pts), f32),
            pltpu.VMEM((rhs_n, pts), f32),
            pltpu.VMEM((7, pts, feat_n), bf16),
            pltpu.VMEM((7, CHUNKS, width // 2 + 16, 128), bf16),
            pltpu.VMEM((7, 8, 128), f32),
            pltpu.VMEM((2, pts, 128), f32),
            pltpu.VMEM((2 * rhs_n, pts), bf16),
            pltpu.VMEM((pts, width), f32),
            pltpu.VMEM((pts, width), f32),
            pltpu.VMEM((pts, 2 * width), bf16),
            pltpu.VMEM((pts, 2 * width), bf16),
            pltpu.VMEM((pts, 128), f32),
            pltpu.VMEM((pts, 128), f32),
            pltpu.VMEM((4, CHUNKS, width // 2 + 16, 128), bf16),
            pltpu.VMEM((4, CHUNKS, width // 2 + 16, 128), bf16),
            pltpu.VMEM((n_sums, 8, 128), f32),
            dma((3,)),
            dma((9, CHUNKS)),
            dma((7, CHUNKS)),
            dma((9, CHUNKS)),
            dma((7, CHUNKS)),
            dma((9,)),
            dma((7,)),
            dma((4, CHUNKS)),
            dma((4, CHUNKS)),
            dma((n_sums,)),
            dma((n_sums,)),
        ],
        compiler_params=pltpu.CompilerParams(
            collective_id=0, has_side_effects=True, vmem_limit_bytes=60 * 1024 * 1024
        ),
        name="cg_step",
    )(features, lengthscale.reshape(1, feat_n), noise_var, outputscale, direction.T, residual.T)
    applied = applied.T
    step_size, ratio = coef[:, 0], coef[:, 128]
    new_solution = solution + step_size[None, :] * direction
    new_residual = residual - step_size[None, :] * applied
    new_direction = new_residual + ratio[None, :] * direction
    return (new_solution, new_residual, new_direction)


def solution(mesh):
    n_dev = mesh.shape[AXIS]
    rows = P(AXIS, None)

    def whole(*arrays):
        return local(n_dev, *arrays)

    return jax.shard_map(
        whole,
        mesh=mesh,
        in_specs=(rows, P(), P(), P(), rows, rows, rows),
        out_specs=(rows, rows, rows),
        check_vma=False,
    )
```

time: 78.3 us -> 65.5 us (0.84)
  the two profiles are of different devices: /device:TPU:12 before, /device:TPU:32 now
where the time goes in v1:
time: 65.5 us; the launch traced here: 65.2 us
  Pallas kernels  60.4 us (92%)
  between operations  1.98 us (3%)
  other arithmetic  1.96 us (3%)
  local copies, waits for them, and re-layouts  0.89 us (1%)
    pallas_call x1, Pallas kernels, local(): pl.pallas_call(body, out_shape=(jax.ShapeDtypeStruct((rhs_n, pts), f32),...  60.4 us
    add x1, other arithmetic, local(): new_direction = new_residual + ratio[None, :] * direction  1.96 us

profile of v1, /device:TPU:32, one launch (start us, length us, event | category | flops | bytes accessed | tf_op | source)
XLA Modules:
  0.0 65.2 jit_solution(5800198665658448681)
XLA Ops:
  1.9 0.0 copy-start
  1.9 0.0 copy-start.1
  1.9 0.0 copy-start.2
  2.0 60.4 %cg_step.1 = (f32[64,1024]{1,0:T(8,128)}, f32[64,256]{1,0:T(8,128)}) custom-call(bf16[1024,128]{1,0:T(8,128)(2,1)} %refs_0_.1, f32[1,128]{1,0:T(1,128)} %bitcast.8, f32[1]{0:T(128)S(6)} %copy.10.refs_2_, f32[1]{0:T(128)S(6)} %copy.11.refs_3_, f32[64,1024]{1,0:T(8,128)} %bitcast.6, f32[64,1024]{1,0:T(8,128)} %bitcast.7), custom_call_target="tpu_custom_call" | custom-call | tf_op jit(solution)/shard_map/cg_step/pallas_call | solution.py:407
  62.4 0.9 %slice_reduce_fusion = (f32[64]{0:T(128)S(1)}, f32[64]{0:T(128)S(1)}) fusion(f32[64,256]{1,0:T(8,128)} %get-tuple-element.5), kind=kLoop, calls=%fused_computation.3 | loop fusion | bytes 1024 | tf_op jit(solution)/shard_map/slice | solution.py:451
  63.2 0.0 copy-done
  63.2 0.0 copy-done.1
  63.3 0.0 copy-done.2
  63.3 2.0 %multiply_add_fusion = (f32[1024,64]{0,1:T(8,128)}, f32[1024,64]{0,1:T(8,128)}, f32[1024,64]{0,1:T(8,128)}) fusion(f32[1024,64]{0,1:T(8,128)S(1)} %copy-done, f32[64]{0:T(128)S(1)} %get-tuple-element.7, f32[1024,64]{0,1:T(8,128)S(1)} %copy-done.1, f32[64,1024]{1,0:T(8,128)} %get-tuple-element.6, f32[64]{0:T(128)S(1)} %get-tuple-element.8, ...), kind=kLoop, calls=%fused_computation.1 | loop fusion | flops 393216 | bytes 1835520 | tf_op jit(solution)/shard_map/add | solution.py:454
Async XLA Ops:
  1.9 61.3 %copy-start = (f32[1024,64]{0,1:T(8,128)S(1)}, f32[1024,64]{0,1:T(8,128)}, u32[]{:S(2)}) copy-start(f32[1024,64]{0,1:T(8,128)} %param.13) | copy-start | bytes 786436
  1.9 61.3 %copy-start.1 = (f32[1024,64]{0,1:T(8,128)S(1)}, f32[1024,64]{0,1:T(8,128)}, u32[]{:S(2)}) copy-start(f32[1024,64]{0,1:T(8,128)} %param.12) | copy-start | bytes 786436
  1.9 61.3 %copy-start.2 = (f32[1024,64]{0,1:T(8,128)S(1)}, f32[1024,64]{0,1:T(8,128)}, u32[]{:S(2)}) copy-start(f32[1024,64]{0,1:T(8,128)} %param.11) | copy-start | bytes 786436

commit v2 on v1

--- a/solution.py
+++ b/solution.py
@@ -28,7 +28,7 @@
 def kernel(
     n_dev, width, features, lengthscale, noise_var, outputscale, direction, residual,
     applied_ref, coef_ref,
-    feat, dvec, res, xbuf, dbuf, meta, half_col, dt, s0, s1, t0, t1, acc, acc2, ret_out, ret_in, sums,
+    feat, dvec, res, xbuf, dbuf, meta, half_col, dt, s0, s1, t0, t1, middle, centre, dsum, acc, acc2, ret_out, ret_in, sums,
     load_sem, x_send, x_recv, d_send, d_recv, m_send, m_recv, r_send, r_recv, a_send, a_recv,
 ):
     me = lax.axis_index(AXIS)
@@ -168,6 +168,7 @@
     exact = scaled.astype(jnp.float32)
     half = 0.5 * jnp.sum(exact * exact, axis=1, keepdims=True)
     half_col[0] = jnp.broadcast_to(half, (pts, 128))
+    middle[0] = jnp.mean(half_col[0], axis=0, keepdims=True)
     for r in range(pts // 128):
         meta[OWN, r : r + 1, :] = half_col[0, r * 128 : (r + 1) * 128, :].T[0:1, :]
     loads[1].wait()
@@ -185,29 +186,34 @@
         rows = pl.ds(pl.multiple_of(chunk * width, width), width)
         s_buf[par][...] = dot(xbuf[left_slot], xbuf[slot, rows, :], ((1,), (1,)))
 
+    def covariance(u):
+        r = u * lax.rsqrt(u)
+        return ((r + POLY_P) * r + POLY_Q) * jnp.exp2(r * (-RATE))
+
     def elem(half_slot, slot, chunk, par):
         for h in range(width // 128):
             row = meta[slot, pl.ds(chunk * (width // 128) + h, 1), :]
+            mid = covariance(jnp.maximum(middle[half_slot] + row, TINY))
+            centre[par, h : h + 1, :] = mid
             for strip in range(pts // STRIP):
                 rows = slice(strip * STRIP, (strip + 1) * STRIP)
                 lanes = slice(h * 128, (h + 1) * 128)
                 u = (half_col[half_slot, rows, :] + row) - s_buf[par][rows, lanes]
-                u = jnp.maximum(u, TINY)
-                r = u * lax.rsqrt(u)
-                value = ((r + POLY_P) * r + POLY_Q) * jnp.exp2(r * (-RATE))
-                top = value.astype(jnp.bfloat16)
-                rest = (value - top.astype(jnp.float32)).astype(jnp.bfloat16)
-                t_buf[par][rows, lanes] = top
-                t_buf[par][rows, slice(width + h * 128, width + (h + 1) * 128)] = rest
+                t_buf[par][rows, lanes] = (covariance(jnp.maximum(u, TINY)) - mid).astype(jnp.bfloat16)
 
     def forward(total, slot, chunk, par):
         both, top = vectors(slot, chunk)
-        total[...] += dot(t_buf[par][...], jnp.concatenate([both, top], axis=0), ((1,), (0,)))
+        mid = jnp.concatenate([centre[par, h : h + 1, :] for h in range(width // 128)], axis=1)
+        mid = jnp.broadcast_to(mid, (16, width))
+        high = mid.astype(jnp.bfloat16)
+        low = (mid - high.astype(jnp.float32)).astype(jnp.bfloat16)
+        added = dot(high, both, ((1,), (0,))) + dot(low, top, ((1,), (0,)))
+        total[...] += dot(t_buf[par][...], both, ((1,), (0,))) + added[0:1]
 
     def backward(kind, chunk, par):
-        full = dot(dt[...], t_buf[par][:, :width], ((1,), (0,)))
-        rest = dot(dt[:rhs_n, :], t_buf[par][:, width:], ((1,), (0,)))
-        code, back = encode(pack_rows(full[:rhs_n] + full[rhs_n:] + rest))
+        full = dot(dt[...], t_buf[par][...], ((1,), (0,)))
+        added = [dsum[...] * centre[par, h : h + 1, :] for h in range(width // 128)]
+        code, back = encode(pack_rows(full[:rhs_n] + full[rhs_n:] + jnp.concatenate(added, axis=1)))
         ret_out[kind, chunk, :part] = code
         ret_out[kind, chunk, part:] = back
 
@@ -227,6 +233,7 @@
 
     def run(left_slot, half_slot, steps, place, total, each_pair=None, kind=None):
         t1[...] = jnp.zeros_like(t1)
+        centre[1] = jnp.zeros_like(centre[1])
         gram(left_slot, *place(0), 0)
 
         @pl.loop(0, steps // 2)
@@ -274,7 +281,7 @@
     run(OWN, 0, 3 * CHUNKS, first_place, acc, first_arrivals)
     pass_on(M1, CHUNKS - 1, False)
 
-    for kind, left_slot, slot, back_to, ahead_to in ((0, M32, P33, 33, -32), (2, M2, P1, 1, -2)):
+    for kind, left_slot, slot, back_to, ahead_to in ((2, M2, P1, 1, -2), (0, M32, P33, 33, -32)):
         for late in (P33,) if kind == 0 else (M2, P1):
             got_meta(late)
             for chunk in range(CHUNKS):
@@ -285,6 +292,9 @@
             ).T
         for chunk in range(CHUNKS):
             dt[:, chunk * width : (chunk + 1) * width] = vectors(left_slot, chunk)[0].T
+        middle[1] = jnp.mean(half_col[1], axis=0, keepdims=True)
+        total_d = jnp.sum(dt[...].astype(jnp.float32), axis=1, keepdims=True)
+        dsum[...] = jnp.broadcast_to(total_d[:rhs_n] + total_d[rhs_n:], (rhs_n, 128))
         acc2[...] = jnp.zeros_like(acc2)
         run(left_slot, 1, CHUNKS, lambda step, slot=slot: (slot, step), acc2, None, kind)
         for chunk in range(CHUNKS):
@@ -362,8 +372,7 @@
     step_size = old_norm / jnp.maximum(curvature, 1.0)
     updated = old_norm - 2.0 * step_size * cross_term + step_size * step_size * applied_norm
     ratio = updated / (old_norm + 1e-6)
-    for i, value in enumerate((step_size, ratio)):
-        coef_ref[:, i * 128 : (i + 1) * 128] = jnp.broadcast_to(value, (128, 128)).T[:rhs_n]
+    coef_ref[...] = jnp.concatenate([step_size, ratio, jnp.zeros((6, 128), jnp.float32)], axis=0)
 
     for way in range(len(ways)):
         def left(way=way):
@@ -408,7 +417,7 @@
         body,
         out_shape=(
             jax.ShapeDtypeStruct((rhs_n, pts), f32),
-            jax.ShapeDtypeStruct((rhs_n, 256), f32),
+            jax.ShapeDtypeStruct((8, 128), f32),
         ),
         in_specs=[in_place, vmem, smem, smem, in_place, in_place],
         out_specs=(vmem, vmem),
@@ -423,8 +432,11 @@
             pltpu.VMEM((2 * rhs_n, pts), bf16),
             pltpu.VMEM((pts, width), f32),
             pltpu.VMEM((pts, width), f32),
-            pltpu.VMEM((pts, 2 * width), bf16),
-            pltpu.VMEM((pts, 2 * width), bf16),
+            pltpu.VMEM((pts, width), bf16),
+            pltpu.VMEM((pts, width), bf16),
+            pltpu.VMEM((2, 1, 128), f32),
+            pltpu.VMEM((2, width // 128, 128), f32),
+            pltpu.VMEM((rhs_n, 128), f32),
             pltpu.VMEM((pts, 128), f32),
             pltpu.VMEM((pts, 128), f32),
             pltpu.VMEM((4, CHUNKS, width // 2 + 16, 128), bf16),
@@ -448,7 +460,7 @@
         name="cg_step",
     )(features, lengthscale.reshape(1, feat_n), noise_var, outputscale, direction.T, residual.T)
     applied = applied.T
-    step_size, ratio = coef[:, 0], coef[:, 128]
+    step_size, ratio = coef[0, :rhs_n], coef[1, :rhs_n]
     new_solution = solution + step_size[None, :] * direction
     new_residual = residual - step_size[None, :] * applied
     new_direction = new_residual + ratio[None, :] * direction

time: 65.5 us -> 63.3 us (0.966)
  Pallas kernels: 60.4 us -> 58.2 us
    pallas_call x1, Pallas kernels: 60.4 us -> 58.2 us  [local(): pl.pallas_call(body, out_shape=(jax.ShapeDtypeStruct((rhs_n, pts), f32),...]
    slice x1 -> x0, local copies, waits for them, and re-layouts: 0.88 us -> none  [local(): step_size, ratio = (coef[:, 0], coef[:, 128])]
    mul x0 -> x1, local copies, waits for them, and re-layouts: none -> 0.75 us  [local(): new_direction = new_residual + ratio[None, :] * direction]
where the time goes in v2:
time: 63.3 us; the launch traced here: 62.9 us
  Pallas kernels  58.2 us (92%)
  other arithmetic  1.96 us (3%)
  between operations  1.96 us (3%)
  local copies, waits for them, and re-layouts  0.76 us (1%)
    pallas_call x1, Pallas kernels, local(): pl.pallas_call(body, out_shape=(jax.ShapeDtypeStruct((rhs_n, pts), f32),...  58.2 us
    add x1, other arithmetic, local(): new_direction = new_residual + ratio[None, :] * direction  1.96 us

profile of v2, /device:TPU:32, one launch (start us, length us, event | category | flops | bytes accessed | tf_op | source)
XLA Modules:
  0.0 62.9 jit_solution(8376255280327380663)
XLA Ops:
  1.9 0.0 copy-start
  1.9 0.0 copy-start.1
  1.9 0.0 copy-start.2
  2.0 58.2 %cg_step.1 = (f32[64,1024]{1,0:T(8,128)}, f32[8,128]{1,0:T(8,128)}) custom-call(bf16[1024,128]{1,0:T(8,128)(2,1)} %refs_0_.1, f32[1,128]{1,0:T(1,128)} %bitcast.12, f32[1]{0:T(128)S(6)} %copy.10.refs_2_, f32[1]{0:T(128)S(6)} %copy.11.refs_3_, f32[64,1024]{1,0:T(8,128)} %bitcast.10, f32[64,1024]{1,0:T(8,128)} %bitcast.11), custom_call_target="tpu_custom_call" | custom-call | tf_op jit(solution)/shard_map/cg_step/pallas_call | solution.py:416
  60.2 0.8 %slice_bitcast_fusion = (f32[64]{0:T(128)S(1)}, f32[64]{0:T(128)S(1)}) fusion(f32[8,128]{1,0:T(8,128)} %get-tuple-element.5), kind=kLoop, calls=%fused_computation.3 | loop fusion | bytes 1024 | tf_op jit(solution)/shard_map/mul | solution.py:466
  60.9 0.0 copy-done
  60.9 0.0 copy-done.1
  60.9 0.0 copy-done.2
  60.9 2.0 %multiply_add_fusion = (f32[1024,64]{0,1:T(8,128)}, f32[1024,64]{0,1:T(8,128)}, f32[1024,64]{0,1:T(8,128)}) fusion(f32[1024,64]{0,1:T(8,128)S(1)} %copy-done, f32[64]{0:T(128)S(1)} %get-tuple-element.10, f32[1024,64]{0,1:T(8,128)S(1)} %copy-done.1, f32[64,1024]{1,0:T(8,128)} %get-tuple-element.6, f32[64]{0:T(128)S(1)} %get-tuple-element.11, ...), kind=kLoop, calls=%fused_computation.1 | loop fusion | flops 393216 | bytes 1835520 | tf_op jit(solution)/shard_map/add | solution.py:466
Async XLA Ops:
  1.9 59.0 %copy-start = (f32[1024,64]{0,1:T(8,128)S(1)}, f32[1024,64]{0,1:T(8,128)}, u32[]{:S(2)}) copy-start(f32[1024,64]{0,1:T(8,128)} %param.13) | copy-start | bytes 786436
  1.9 59.0 %copy-start.1 = (f32[1024,64]{0,1:T(8,128)S(1)}, f32[1024,64]{0,1:T(8,128)}, u32[]{:S(2)}) copy-start(f32[1024,64]{0,1:T(8,128)} %param.12) | copy-start | bytes 786436
  1.9 59.0 %copy-start.2 = (f32[1024,64]{0,1:T(8,128)S(1)}, f32[1024,64]{0,1:T(8,128)}, u32[]{:S(2)}) copy-start(f32[1024,64]{0,1:T(8,128)} %param.11) | copy-start | bytes 786436

commit v3 on v2

--- a/solution.py
+++ b/solution.py
@@ -281,7 +281,7 @@
     run(OWN, 0, 3 * CHUNKS, first_place, acc, first_arrivals)
     pass_on(M1, CHUNKS - 1, False)
 
-    for kind, left_slot, slot, back_to, ahead_to in ((2, M2, P1, 1, -2), (0, M32, P33, 33, -32)):
+    for kind, left_slot, slot, back_to, ahead_to in ((0, M32, P33, 33, -32), (2, M2, P1, 1, -2)):
         for late in (P33,) if kind == 0 else (M2, P1):
             got_meta(late)
             for chunk in range(CHUNKS):

time: 63.3 us -> 61.3 us (0.968)
  Pallas kernels: 58.2 us -> 56.4 us
    pallas_call x1, Pallas kernels: 58.2 us -> 56.4 us  [local(): pl.pallas_call(body, out_shape=(jax.ShapeDtypeStruct((rhs_n, pts), f32),...]
where the time goes in v3:
time: 61.3 us; the launch traced here: 61.1 us
  Pallas kernels  56.4 us (92%)
  other arithmetic  1.96 us (3%)
  between operations  1.96 us (3%)
  local copies, waits for them, and re-layouts  0.76 us (1%)
    pallas_call x1, Pallas kernels, local(): pl.pallas_call(body, out_shape=(jax.ShapeDtypeStruct((rhs_n, pts), f32),...  56.4 us
    add x1, other arithmetic, local(): new_direction = new_residual + ratio[None, :] * direction  1.96 us

profile of v3, /device:TPU:32, one launch (start us, length us, event | category | flops | bytes accessed | tf_op | source)
XLA Modules:
  0.0 61.1 jit_solution(15292375072011960108)
XLA Ops:
  1.9 0.0 copy-start
  1.9 0.0 copy-start.1
  1.9 0.0 copy-start.2
  2.0 56.4 %cg_step.1 = (f32[64,1024]{1,0:T(8,128)}, f32[8,128]{1,0:T(8,128)}) custom-call(bf16[1024,128]{1,0:T(8,128)(2,1)} %refs_0_.1, f32[1,128]{1,0:T(1,128)} %bitcast.12, f32[1]{0:T(128)S(6)} %copy.10.refs_2_, f32[1]{0:T(128)S(6)} %copy.11.refs_3_, f32[64,1024]{1,0:T(8,128)} %bitcast.10, f32[64,1024]{1,0:T(8,128)} %bitcast.11), custom_call_target="tpu_custom_call" | custom-call | tf_op jit(solution)/shard_map/cg_step/pallas_call | solution.py:416
  58.4 0.8 %slice_bitcast_fusion = (f32[64]{0:T(128)S(1)}, f32[64]{0:T(128)S(1)}) fusion(f32[8,128]{1,0:T(8,128)} %get-tuple-element.5), kind=kLoop, calls=%fused_computation.3 | loop fusion | bytes 1024 | tf_op jit(solution)/shard_map/mul | solution.py:466
  59.1 0.0 copy-done
  59.1 0.0 copy-done.1
  59.1 0.0 copy-done.2
  59.1 2.0 %multiply_add_fusion = (f32[1024,64]{0,1:T(8,128)}, f32[1024,64]{0,1:T(8,128)}, f32[1024,64]{0,1:T(8,128)}) fusion(f32[1024,64]{0,1:T(8,128)S(1)} %copy-done, f32[64]{0:T(128)S(1)} %get-tuple-element.10, f32[1024,64]{0,1:T(8,128)S(1)} %copy-done.1, f32[64,1024]{1,0:T(8,128)} %get-tuple-element.6, f32[64]{0:T(128)S(1)} %get-tuple-element.11, ...), kind=kLoop, calls=%fused_computation.1 | loop fusion | flops 393216 | bytes 1835520 | tf_op jit(solution)/shard_map/add | solution.py:466
Async XLA Ops:
  1.9 57.2 %copy-start = (f32[1024,64]{0,1:T(8,128)S(1)}, f32[1024,64]{0,1:T(8,128)}, u32[]{:S(2)}) copy-start(f32[1024,64]{0,1:T(8,128)} %param.13) | copy-start | bytes 786436
  1.9 57.2 %copy-start.1 = (f32[1024,64]{0,1:T(8,128)S(1)}, f32[1024,64]{0,1:T(8,128)}, u32[]{:S(2)}) copy-start(f32[1024,64]{0,1:T(8,128)} %param.12) | copy-start | bytes 786436
  1.9 57.2 %copy-start.2 = (f32[1024,64]{0,1:T(8,128)S(1)}, f32[1024,64]{0,1:T(8,128)}, u32[]{:S(2)}) copy-start(f32[1024,64]{0,1:T(8,128)} %param.11) | copy-start | bytes 786436
